TPU v7x, 256 devices: a whole 4x4x8 slice. The times are simulated.
256 devices in a mesh: level: 2 (over core), gx: 4 (over x), yz: 32 (over z, y).
Axes of the slice: x: 4, y: 4, z: 8, core: 2. Of those that a mesh axis runs over, the one named last changes fastest.
Arguments:
- init_field: float32 [128, 512, 256], P('gx', 'yz'), may hold values from -6 to 6
- source: float32 [128, 512, 256], P('gx', 'yz'), may hold values from -4 to 4
- damping: float32 [128, 512, 256], P('gx', 'yz'), may hold values from 0.05 to 2
Outputs:
- final_states: float32 [2, 128, 512, 256], P('level', 'gx', 'yz')
All inputs are finite; a program needn't handle non-finite values.
Results may differ from a plain program's by a relative error of at most 0.0001.
Values sent between devices are 32-bit elements; how exact they have to be, the bound alone decides.
A program may use at most 64 MiB of HBM per device.

v0:
```python
import functools

import jax
import jax.numpy as jnp
from jax import lax
from jax.experimental import pallas as pl
from jax.experimental.pallas import tpu as pltpu
from jax.sharding import PartitionSpec as P

STEPS = 3
ITERS = 3
PX = 3
PY = 8
LANES = 128
MID = 8.025
HALF = 6.975
MESH = pl.DeviceIdType.MESH
DIRS = ((-1, 0), (1, 0), (0, -1), (0, 1), (-1, -1), (-1, 1), (1, -1), (1, 1))


def times_a(c):
    out = [MID * v for v in c] + [jnp.zeros_like(c[0])]
    for k, v in enumerate(c):
        if k == 0:
            out[1] = out[1] + HALF * v
        else:
            out[k + 1] = out[k + 1] + (0.5 * HALF) * v
            out[k - 1] = out[k - 1] + (0.5 * HALF) * v
    return out


def plus(a, b):
    short, long = (a, b) if len(a) < len(b) else (b, a)
    return [x + y for x, y in zip(short, long)] + long[len(short):]


def scaled(s, a):
    return [s * x for x in a]


def cg_coefficients(dots):
    m = [dots[0], dots[1], 2.0 * dots[2] - dots[0], 2.0 * dots[3] - dots[1],
         2.0 * dots[4] - dots[0], 2.0 * dots[5] - dots[1]]

    def inner(a, b):
        total = None
        for i, x in enumerate(a):
            for j, y in enumerate(b):
                term = (x * y) * (0.5 * (m[i + j] + m[abs(i - j)]))
                total = term if total is None else total + term
        return total

    one = jnp.ones_like(m[0])
    resid = [one]
    direction = resid
    image = times_a(resid)
    along = image
    norm_now = m[0]
    alpha = norm_now / inner(resid, image)
    answer = None
    for step in range(ITERS):
        move = scaled(alpha, direction)
        answer = move if answer is None else plus(answer, move)
        if step + 1 < ITERS:
            resid = plus(resid, scaled(-alpha, along))
            image = times_a(resid)
            norm_next = inner(resid, resid)
            product = inner(resid, image)
            ratio = norm_next / norm_now
            alpha = norm_next / (product - ratio * norm_next / alpha)
            direction = plus(resid, scaled(ratio, direction))
            along = plus(image, scaled(ratio, along))
            norm_now = norm_next
    change = plus(times_a(answer), scaled(-1.0, answer))
    return answer, change


def body(sizes, stages, init_ref, source_ref, damp_ref, out_ref, p0, src, dmp, heads_p, heads_c,
         work_p, work_c, ahead, base, sums, result, inbox, slots, in_sem, send_sem, recv_sem, red_send, red_recv, out_sem):
    levels, nx, ny = sizes
    half = src.shape[0]
    parts = src.shape[1]
    rows = src.shape[2]
    level, gx, yz = lax.axis_index("level"), lax.axis_index("gx"), lax.axis_index("yz")
    xpos = gx * levels + level
    xcount = nx * levels
    x_in = (xpos > 0, xpos < xcount - 1)
    y_in = (yz > 0, yz < ny - 1)

    def exists(dx, dy):
        ok = None
        for d, pair in ((dx, x_in), (dy, y_in)):
            if d != 0:
                c = pair[0] if d < 0 else pair[1]
                ok = c if ok is None else jnp.logical_and(ok, c)
        return ok

    mine = pl.ds(level * half, half)
    loads = []
    for i, (ref, buf, pad) in enumerate(((init_ref, p0, True), (damp_ref, dmp, True), (source_ref, src, False))):
        for z in range(parts):
            lanes = slice(z * LANES, (z + 1) * LANES)
            dst = buf.at[PX:PX + half, z, PY:PY + rows, :] if pad else buf.at[:, z, :, :]
            copy = pltpu.make_async_copy(ref.at[mine, :, lanes], dst, in_sem.at[i, z])
            copy.start()
            loads.append(copy)

    zero_x = jnp.zeros((PX,) + tuple(p0.shape[1:]), jnp.float32)
    zero_y = jnp.zeros((p0.shape[0], parts, PY, LANES), jnp.float32)
    for buf in [p0] + [h.at[n] for h in (heads_p, heads_c) for n in range(STEPS)]:
        @pl.when(jnp.logical_not(x_in[0]))
        def _(buf=buf):
            buf[0:PX] = zero_x

        @pl.when(jnp.logical_not(x_in[1]))
        def _(buf=buf):
            buf[PX + half:] = zero_x

        @pl.when(jnp.logical_not(y_in[0]))
        def _(buf=buf):
            buf[:, :, 0:PY, :] = zero_y

        @pl.when(jnp.logical_not(y_in[1]))
        def _(buf=buf):
            buf[:, :, PY + rows:, :] = zero_y

    def halo_copy(buf, width, slot, k, into=None):
        dx, dy = DIRS[k]
        w = width if 0 in (dx, dy) else width - 1
        if w == 0:
            return None

        def spans(d, pad, size):
            if d == 0:
                return slice(pad, pad + size), slice(pad, pad + size)
            if d < 0:
                return slice(pad, pad + w), slice(pad + size, pad + size + w)
            return slice(pad + size - w, pad + size), slice(pad - w, pad)

        sx, tx = spans(dx, PX, half)
        sy, ty = spans(dy, PY, rows)
        to = xpos + dx
        return pltpu.make_async_remote_copy(
            src_ref=buf.at[sx, :, sy, :], dst_ref=(buf if into is None else into).at[tx, :, ty, :],
            send_sem=send_sem.at[slot, k], recv_sem=recv_sem.at[slot, k],
            device_id={"level": lax.rem(to + levels, levels), "gx": lax.div(to + levels, levels) - 1, "yz": yz + dy},
            device_id_type=MESH,
        )

    order = (4, 5, 6, 7, 2, 3, 0, 1)

    def send_halo(buf, width, slot, into=None):
        for k in order:
            copy = halo_copy(buf, width, slot, k, into)
            if copy is not None:
                pl.when(exists(*DIRS[k]))(lambda copy=copy: copy.start())

    def wait_halo(buf, width, slot, into=None):
        for k in order:
            copy = halo_copy(buf, width, slot, k, into)
            if copy is not None:
                dx, dy = DIRS[k]
                pl.when(exists(-dx, -dy))(lambda copy=copy: copy.wait_recv())

    def end_halo(buf, width, slot, into=None):
        for k in order:
            copy = halo_copy(buf, width, slot, k, into)
            if copy is not None:
                pl.when(exists(*DIRS[k]))(lambda copy=copy: copy.wait_send())

    def stencil(v, x, start, count):
        lane = lax.broadcasted_iota(jnp.int32, (count, LANES), 1)
        own = pl.ds(start, count)
        centre = [v[x, z, own, :] for z in range(parts)]
        fore = [pltpu.roll(c, 1, 1) for c in centre]
        back = [pltpu.roll(c, LANES - 1, 1) for c in centre]
        out = []
        for z in range(parts):
            near = jnp.where(lane == 0, fore[z - 1] if z > 0 else 0.0, fore[z])
            far = jnp.where(lane == LANES - 1, back[z + 1] if z + 1 < parts else 0.0, back[z])
            beside = v[x - 1, z, own, :] + v[x + 1, z, own, :]
            beside = beside + v[x, z, pl.ds(start - 1, count), :] + v[x, z, pl.ds(start + 1, count), :]
            beside = beside + (near + far)
            out.append((dmp[x, z, own, :] + (7.0 - MID)) * centre[z] - beside)
        return out, centre

    low = jnp.where(y_in[0], 0, PY)
    high = jnp.where(y_in[1], 2 * PY + rows, PY + rows)

    def fold(block):
        return jnp.sum(block.reshape(-1, 8, LANES), axis=0)

    def powers(head, work):
        zero = jnp.zeros((8, LANES), jnp.float32)
        own = pl.ds(PY, rows)
        totals = []
        for k in range(1, ITERS + 1):
            h = ITERS - k
            start = PY - h
            count = -(-(rows + 2 * h) // 8) * 8
            prev = head if k == 1 else work.at[k - 2]
            row = lax.broadcasted_iota(jnp.int32, (count, LANES), 0) + start

            mask = jnp.logical_and(row >= low, row < high)
            keep = jnp.logical_and(row >= PY, row < PY + rows)
            older = None if k == 1 else head if k == 2 else work.at[k - 3]

            def plane(x, inner, sides, k=k, h=h, start=start, count=count, prev=prev, mask=mask, keep=keep, older=older):
                a, b = sides
                t, centre = stencil(prev, x, start, count)
                ok = mask
                if not inner:
                    ok = jnp.logical_and(mask, x_in[0] if x < PX else x_in[1])
                for z in range(parts):
                    if k == 1:
                        new = t[z] * (1.0 / HALF)
                    else:
                        new = t[z] * (2.0 / HALF) - older[x, z, pl.ds(start, count), :]
                    if h > 0:
                        new = jnp.where(ok, new, 0.0)
                    work[k - 1, x, z, pl.ds(start, count), :] = new
                    if inner:
                        square, cross = centre[z] * centre[z], centre[z] * new
                        if h > 0:
                            square, cross = jnp.where(keep, square, 0.0), jnp.where(keep, cross, 0.0)
                        a = a + fold(square)
                        b = b + fold(cross)
                return a, b

            sides = (zero, zero)
            for x in range(PX - h, PX + half + h):
                sides = plane(x, PX <= x < PX + half, sides)
            totals += sides
        return totals

    def position(axes):
        flat = 0
        for a in axes:
            flat = flat * lax.axis_size(a) + lax.axis_index(a)
        return flat

    def reduce_all(accs, turn, meanwhile):
        n = len(accs)
        size = -(-n // 8) * 8
        eye = lax.broadcasted_iota(jnp.int32, (size, LANES), 0) == lax.broadcasted_iota(jnp.int32, (size, LANES), 1)
        tall = jnp.concatenate([jnp.sum(a, axis=0, keepdims=True) for a in accs]
                               + [jnp.zeros((size - n, LANES), jnp.float32)] * (size > n), axis=0)
        col = jnp.sum(tall, axis=1, keepdims=True)
        line = jnp.sum(jnp.where(eye, col, 0.0), axis=0, keepdims=True)
        for s, axes in enumerate(stages):
            count = 1
            for a in axes:
                count *= lax.axis_size(a)
            me = position(axes)
            cell = slots[s].at[turn, pl.ds(me, 1), :]
            cell[...] = line
            copies = []
            for off in range(1, count):
                peer = lax.rem(me + off, count)
                ids = {}
                for a in reversed(axes):
                    ids[a] = lax.rem(peer, lax.axis_size(a))
                    peer = lax.div(peer, lax.axis_size(a))
                copy = pltpu.make_async_remote_copy(
                    src_ref=cell, dst_ref=cell, send_sem=red_send[s].at[turn, off - 1],
                    recv_sem=red_recv[s].at[turn, off - 1], device_id=ids, device_id_type=MESH)
                copy.start()
                copies.append(copy)
            if s == 0:
                for item in meanwhile:
                    send_halo(*item)
            for copy in copies:
                copy.wait_recv()
            line = jnp.sum(slots[s][turn], axis=0, keepdims=True)
            for copy in copies:
                copy.wait_send()
        col = jnp.sum(jnp.where(eye, line, 0.0), axis=1, keepdims=True)
        wide = jnp.broadcast_to(col, (size, LANES))
        return [wide[k:k + 1, :] for k in range(n)]

    def to_out(block, part, row):
        return [pltpu.make_async_copy(
            block.at[:, z, :, :], out_ref.at[0, pl.ds(part * half, half), :, slice(z * LANES, (z + 1) * LANES)],
            out_sem.at[row, z]) for z in range(parts)]

    def pieces(f):
        return to_out(result.at[f], level, 2)

    def across(f):
        return pltpu.make_async_remote_copy(
            src_ref=result.at[f], dst_ref=inbox, send_sem=out_sem.at[0, 0], recv_sem=out_sem.at[1, 0],
            device_id={"level": f, "gx": gx, "yz": yz}, device_id_type=MESH)

    def deliver(f):
        pl.when(level != f)(lambda: across(f).start())
        for copy in pieces(f):
            pl.when(level == f)(lambda copy=copy: copy.start())

    own = pl.ds(PY, rows)
    for copy in loads[:2 * parts]:
        copy.wait()
    send_halo(p0, 1, 0)
    send_halo(dmp, ITERS - 1, 1)
    for copy in loads[2 * parts:]:
        copy.wait()
    wait_halo(p0, 1, 0)

    def start_plane(x, carry):
        t, centre = stencil(p0, x, PY, rows)
        for z in range(parts):
            r = src[x - PX, z] - (t[z] + (MID - 1.0) * centre[z])
            heads_p[0, x, z, own, :] = r
            base[x - PX, z] = r
        return carry

    lax.fori_loop(PX, PX + half, start_plane, 0, unroll=True)

    pending = [(p0, 1, 0), (dmp, ITERS - 1, 1)]
    slot = 2
    for turn in range(STEPS + 1):
        with_p, with_c = turn < STEPS, turn > 0
        fields = []
        if with_p:
            fields.append((heads_p.at[turn], work_p))
        if with_c:
            fields.append((heads_c.at[turn - 1], work_c))
        slots_here = []
        for head, _ in fields:
            if turn != 1:
                send_halo(head, ITERS, slot)
                slots_here.append((head, ITERS, slot))
                slot += 1
        if turn == 0:
            wait_halo(dmp, ITERS - 1, 1)
        accs = []
        for i, (head, work) in enumerate(fields):
            if turn != 1:
                wait_halo(*slots_here[i])
            accs += powers(head, work)
        pending += slots_here
        outer = []
        if turn == 0:
            for k in range(ITERS):
                outer.append((work_p.at[k], ITERS, slot, ahead.at[k]))
                slot += 1
            pending += outer
        dots = reduce_all(accs, turn, outer)
        coeff = [cg_coefficients(dots[6 * i:6 * i + 6]) for i in range(len(fields))]

        def update(i, carry, turn=turn, with_p=with_p, with_c=with_c, fields=fields, coeff=coeff):
            x = i + PX

            def basis(f, z):
                head, work = fields[f]
                return [head[x, z, own, :]] + [work[k, x, z, own, :] for k in range(ITERS)]

            def combine(c, v):
                total = c[0] * v[0]
                for a, b in zip(c[1:], v[1:]):
                    total = total + a * b
                return total

            for z in range(parts):
                line = base[i, z] if turn < STEPS else None
                if with_p:
                    v = basis(0, z)
                    rise = combine(coeff[0][0], v)
                    change = combine(coeff[0][1], v)
                    before = p0[x, z, own, :] if turn == 0 else sums[0, i, z]
                    if turn + 1 < STEPS:
                        sums[0, i, z] = before + rise
                        heads_p[turn + 1, x, z, own, :] = v[0] - change
                    else:
                        result[0, i, z] = before + rise
                if with_c:
                    v = basis(len(fields) - 1, z)
                    rise = combine(coeff[-1][0], v)
                    before = p0[x, z, own, :] if turn == 1 else sums[1, i, z]
                    if turn < STEPS:
                        sums[1, i, z] = before + rise
                        line = line - combine(coeff[-1][1], v)
                        base[i, z] = line
                    else:
                        result[1, i, z] = before + rise
                if turn < STEPS:
                    heads_c[turn, x, z, own, :] = line + 0.5 * change
            return carry

        lax.fori_loop(0, half, update, 0, unroll=True)
        if turn == 0:
            for item in outer:
                wait_halo(*item)
                end_halo(*item)
            pending = pending[:-len(outer)]

            def rim(x, begin, count, plane_ok):
                span = pl.ds(begin, count)
                row = lax.broadcasted_iota(jnp.int32, (count, LANES), 0) + begin
                ok = jnp.logical_and(row >= low, row < high)
                if plane_ok is not None:
                    ok = jnp.logical_and(ok, plane_ok)
                for z in range(parts):
                    now = heads_p[0, x, z, span, :]
                    change = coeff[0][1][0] * now
                    for k in range(ITERS):
                        change = change + coeff[0][1][k + 1] * ahead[k, x, z, span, :]
                    heads_p[1, x, z, span, :] = jnp.where(ok, now - change, 0.0)
                    heads_c[0, x, z, span, :] = jnp.where(ok, now + 0.5 * change, 0.0)

            for x in range(PX):
                rim(x, 0, 2 * PY + rows, x_in[0])
                rim(PX + half + x, 0, 2 * PY + rows, x_in[1])
            for x in range(PX, PX + half):
                rim(x, 0, PY, None)
                rim(x, PY + rows, PY, None)
        if turn == STEPS - 1:
            deliver(0)
    deliver(1)

    for item in pending:
        end_halo(*item)
    for f in range(2):
        pl.when(level != f)(lambda f=f: across(f).wait_send())
        pl.when(level == f)(lambda f=f: across(f).wait_recv())
        for copy in pieces(f):
            pl.when(level == f)(lambda copy=copy: copy.wait())
    ends = to_out(inbox, 1 - level, 3)
    for copy in ends:
        copy.start()
    for copy in ends:
        copy.wait()


def solution(mesh):
    levels, nx, ny = mesh.shape["level"], mesh.shape["gx"], mesh.shape["yz"]
    if levels * nx * ny <= 64:
        stages = (("level", "gx", "yz"),)
    else:
        stages = (("level", "gx"), ("yz",))

    def per_device(init_field, source, damping):
        deep, rows, wide = init_field.shape
        half, parts = deep // levels, wide // LANES
        padded = (half + 2 * PX, parts, rows + 2 * PY, LANES)
        plain = (half, parts, rows, LANES)
        counts = []
        for axes in stages:
            n = 1
            for a in axes:
                n *= mesh.shape[a]
            counts.append(n)
        turns = STEPS + 1
        dma = pltpu.SemaphoreType.DMA
        exchanges = 2 + 2 * STEPS + ITERS
        return pl.pallas_call(
            functools.partial(body, (levels, nx, ny), stages),
            out_shape=jax.ShapeDtypeStruct((1, deep, rows, wide), jnp.float32),
            in_specs=[pl.BlockSpec(memory_space=pl.ANY)] * 3,
            out_specs=pl.BlockSpec(memory_space=pl.ANY),
            scratch_shapes=[
                pltpu.VMEM(padded, jnp.float32),
                pltpu.VMEM(plain, jnp.float32),
                pltpu.VMEM(padded, jnp.float32),
                pltpu.VMEM((STEPS,) + padded, jnp.float32),
                pltpu.VMEM((STEPS,) + padded, jnp.float32),
                pltpu.VMEM((ITERS,) + padded, jnp.float32),
                pltpu.VMEM((ITERS,) + padded, jnp.float32),
                pltpu.VMEM((ITERS,) + padded, jnp.float32),
                pltpu.VMEM(plain, jnp.float32),
                pltpu.VMEM((2,) + plain, jnp.float32),
                pltpu.VMEM((2,) + plain, jnp.float32),
                pltpu.VMEM(plain, jnp.float32),
                [pltpu.VMEM((turns, n, LANES), jnp.float32) for n in counts],
                dma((3, parts)),
                dma((exchanges, 8)),
                dma((exchanges, 8)),
                [dma((turns, n - 1)) for n in counts],
                [dma((turns, n - 1)) for n in counts],
                dma((4, parts)),
            ],
            compiler_params=pltpu.CompilerParams(has_side_effects=True),
        )(init_field, source, damping)

    spec = P("gx", "yz", None)
    return jax.shard_map(
        per_device, mesh=mesh, in_specs=(spec, spec, spec),
        out_specs=P("level", "gx", "yz", None), check_vma=False,
    )
```

profile of v0, /device:TPU:1, one launch (start us, length us, event | category | flops | bytes accessed | tf_op | source)
XLA Modules:
  0.0 88.3 jit_solution(3953663481225510549)
XLA Ops:
  0.0 86.4 %shard_map.37 = f32[1,32,16,256]{3,2,1,0:T(8,128)} custom-call(f32[32,16,256]{2,1,0:T(8,128)} %init_ref.1, f32[32,16,256]{2,1,0:T(8,128)} %source_ref.1, f32[32,16,256]{2,1,0:T(8,128)} %damp_ref.1), custom_call_target="tpu_custom_call" | custom-call | tf_op jit(solution)/shard_map/pallas_call | solution.py:455
  86.4 1.9 %copy.5 = f32[1,32,16,256]{3,2,1,0:T(8,128)} copy(f32[1,32,16,256]{3,2,1,0:T(8,128)} %shard_map.37) | data formatting | bytes 1048576
where the time goes:
time: 88.5 us; the launch traced here: 88.3 us
  Pallas kernels  86.4 us (98%)
  local copies, waits for them, and re-layouts  1.87 us (2%)
    pallas_call x1, Pallas kernels, per_device(): pl.pallas_call(functools.partial(body, (levels, nx, ny), stages), out_sha...  86.4 us
    unnamed x1, local copies, waits for them, and re-layouts  1.87 us

commit v1 on v0

v1 whole, which is shorter than its diff:
```python
import functools

import jax
import jax.numpy as jnp
from jax import lax
from jax.experimental import pallas as pl
from jax.experimental.pallas import tpu as pltpu
from jax.sharding import PartitionSpec as P

STEPS = 3
ITERS = 3
ROUNDS = (3, 5)
PX = 4
PY = 8
LANES = 128
MID = 8.025
HALF = 6.975
MESH = pl.DeviceIdType.MESH
DIRS = ((-1, 0), (1, 0), (0, -1), (0, 1), (-1, -1), (-1, 1), (1, -1), (1, 1))


def times_a(c):
    out = [MID * v for v in c] + [jnp.zeros_like(c[0])]
    for k, v in enumerate(c):
        if k == 0:
            out[1] = out[1] + HALF * v
        else:
            out[k + 1] = out[k + 1] + (0.5 * HALF) * v
            out[k - 1] = out[k - 1] + (0.5 * HALF) * v
    return out


def plus(a, b):
    short, long = (a, b) if len(a) < len(b) else (b, a)
    return [x + y for x, y in zip(short, long)] + long[len(short):]


def scaled(s, a):
    return [s * x for x in a]


def cg_coefficients(dots):
    m = [dots[0], dots[1], 2.0 * dots[2] - dots[0], 2.0 * dots[3] - dots[1],
         2.0 * dots[4] - dots[0], 2.0 * dots[5] - dots[1]]

    def inner(a, b):
        total = None
        for i, x in enumerate(a):
            for j, y in enumerate(b):
                term = (x * y) * (0.5 * (m[i + j] + m[abs(i - j)]))
                total = term if total is None else total + term
        return total

    one = jnp.ones_like(m[0])
    resid = [one]
    direction = resid
    image = times_a(resid)
    along = image
    norm_now = m[0]
    alpha = norm_now / inner(resid, image)
    answer = None
    for step in range(ITERS):
        move = scaled(alpha, direction)
        answer = move if answer is None else plus(answer, move)
        if step + 1 < ITERS:
            resid = plus(resid, scaled(-alpha, along))
            image = times_a(resid)
            norm_next = inner(resid, resid)
            product = inner(resid, image)
            ratio = norm_next / norm_now
            alpha = norm_next / (product - ratio * norm_next / alpha)
            direction = plus(resid, scaled(ratio, direction))
            along = plus(image, scaled(ratio, along))
            norm_now = norm_next
    change = plus(times_a(answer), scaled(-1.0, answer))
    return answer, change


def shifted(change):
    table = []
    for j in range(ITERS + 1):
        row = [None] * (2 * ITERS + 1)
        for i, c in enumerate(change):
            for l in (i + j, abs(i - j)):
                row[l] = 0.5 * c if row[l] is None else row[l] + 0.5 * c
        for l in range(1, ITERS + 1):
            far = row[ITERS + l]
            if far is not None:
                near = row[ITERS - l]
                row[ITERS - l] = -far if near is None else near - far
                row[ITERS + l] = 2.0 * far
        table.append(row)
    return table


def combine(c, v):
    total = None
    for a, b in zip(c, v):
        if a is not None:
            total = a * b if total is None else total + a * b
    return total


def body(sizes, stages, init_ref, source_ref, damp_ref, out_ref, p0, src, dmp, first, heads_p, heads_c, own_p, own_c,
         base, work_p, work_c, sums, result, slots, in_sem, send_sem, recv_sem, red_send, red_recv, out_sem, p_send, p_recv,
         meet_x, meet_y):
    levels, nx, ny = sizes
    half = own_p.shape[1]
    parts = p0.shape[1]
    rows = own_p.shape[3]
    level, gx, yz = lax.axis_index("level"), lax.axis_index("gx"), lax.axis_index("yz")
    xpos = gx * levels + level
    xcount = nx * levels
    x_in = (xpos > 0, xpos < xcount - 1)
    y_in = (yz > 0, yz < ny - 1)

    def exists(dx, dy):
        ok = None
        for d, at, count in ((dx, xpos, xcount), (dy, yz, ny)):
            if d != 0:
                c = at + d >= 0 if d < 0 else at + d < count
                ok = c if ok is None else jnp.logical_and(ok, c)
        return ok

    def beside(dx, dy):
        to = xpos + dx
        return {"level": lax.rem(to + xcount, levels), "gx": lax.div(to + xcount, levels) - nx, "yz": yz + dy}

    mine = pl.ds(level * half, half)
    loads = []
    for i, (ref, buf) in enumerate(((init_ref, p0), (source_ref, src), (damp_ref, dmp))):
        for z in range(parts):
            copy = pltpu.make_async_copy(ref.at[mine, :, slice(z * LANES, (z + 1) * LANES)],
                                         buf.at[PX:PX + half, z, PY:PY + rows, :], in_sem.at[i, z])
            copy.start()
            loads.append(copy)

    def signal_all(sem, steps):
        count = 0
        for dx, dy in steps:
            ok = exists(dx, dy)
            count = count + jnp.where(ok, 1, 0)

            @pl.when(ok)
            def _(dx=dx, dy=dy):
                pl.semaphore_signal(sem, inc=1, device_id=beside(dx, dy), device_id_type=MESH)
        return count

    def meet(turn):
        if turn > 0:
            for sem, rounds, axis in ((meet_x, ROUNDS[0], 0), (meet_y, ROUNDS[1], 1)):
                if turn <= rounds:
                    far = 2 ** (turn - 1)
                    count = 0
                    for d in (-far, far):
                        count = count + jnp.where(exists(*((d, 0) if axis == 0 else (0, d))), 1, 0)
                    pl.semaphore_wait(sem.at[turn - 1], count)
        for sem, rounds, axis in ((meet_x, ROUNDS[0], 0), (meet_y, ROUNDS[1], 1)):
            if turn < rounds:
                far = 2 ** turn
                signal_all(sem.at[turn], [(d, 0) if axis == 0 else (0, d) for d in (-far, far)])

    barrier = pltpu.get_barrier_semaphore()
    greeted = signal_all(barrier, DIRS)

    zero_x = jnp.zeros((PX,) + tuple(p0.shape[1:]), jnp.float32)
    zero_y = jnp.zeros((p0.shape[0], parts, PY, LANES), jnp.float32)
    for buf in [p0] + [heads_p.at[n] for n in range(STEPS)] + [heads_c.at[n] for n in range(STEPS - 1)]:
        @pl.when(jnp.logical_not(x_in[0]))
        def _(buf=buf):
            buf[0:PX] = zero_x

        @pl.when(jnp.logical_not(x_in[1]))
        def _(buf=buf):
            buf[PX + half:] = zero_x

        @pl.when(jnp.logical_not(y_in[0]))
        def _(buf=buf):
            buf[:, :, 0:PY, :] = zero_y

        @pl.when(jnp.logical_not(y_in[1]))
        def _(buf=buf):
            buf[:, :, PY + rows:, :] = zero_y

    def halo_copy(buf, width, slot, k):
        dx, dy = DIRS[k]
        w = width if 0 in (dx, dy) else width - 1

        def spans(d, pad, size):
            if d == 0:
                return slice(pad, pad + size), slice(pad, pad + size)
            if d < 0:
                return slice(pad, pad + w), slice(pad + size, pad + size + w)
            return slice(pad + size - w, pad + size), slice(pad - w, pad)

        sx, tx = spans(dx, PX, half)
        sy, ty = spans(dy, PY, rows)
        return pltpu.make_async_remote_copy(
            src_ref=buf.at[sx, :, sy, :], dst_ref=buf.at[tx, :, ty, :],
            send_sem=send_sem.at[slot, k], recv_sem=recv_sem.at[slot, k],
            device_id=beside(dx, dy), device_id_type=MESH,
        )

    order = (2, 3, 4, 5, 6, 7, 0, 1)

    def send_halo(*item):
        for k in order:
            pl.when(exists(*DIRS[k]))(lambda k=k: halo_copy(*item, k).start())

    def wait_halo(*item):
        for k in order:
            dx, dy = DIRS[k]
            pl.when(exists(-dx, -dy))(lambda k=k: halo_copy(*item, k).wait_recv())

    def end_halo(*item):
        for k in order:
            pl.when(exists(*DIRS[k]))(lambda k=k: halo_copy(*item, k).wait_send())

    def stencil(v, x, start, count):
        lane = lax.broadcasted_iota(jnp.int32, (count, LANES), 1)
        own = pl.ds(start, count)
        centre = [v[x, z, own, :] for z in range(parts)]
        fore = [pltpu.roll(c, 1, 1) for c in centre]
        back = [pltpu.roll(c, LANES - 1, 1) for c in centre]
        out = []
        for z in range(parts):
            near = jnp.where(lane == 0, fore[z - 1] if z > 0 else 0.0, fore[z])
            far = jnp.where(lane == LANES - 1, back[z + 1] if z + 1 < parts else 0.0, back[z])
            beside = v[x - 1, z, own, :] + v[x + 1, z, own, :]
            beside = beside + v[x, z, pl.ds(start - 1, count), :] + v[x, z, pl.ds(start + 1, count), :]
            beside = beside + (near + far)
            out.append((dmp[x, z, own, :] + (7.0 - MID)) * centre[z] - beside)
        return out, centre

    low = jnp.where(y_in[0], 0, PY)
    high = jnp.where(y_in[1], 2 * PY + rows, PY + rows)

    def fold(block):
        return jnp.sum(block.reshape(-1, 8, LANES), axis=0)

    def reach(h):
        return PY - h, -(-(rows + 2 * h) // 8) * 8

    def inside(x, start, count):
        row = lax.broadcasted_iota(jnp.int32, (count, LANES), 0) + start
        ok = jnp.logical_and(row >= low, row < high)
        if PX <= x < PX + half:
            return ok
        return jnp.logical_and(ok, x_in[0] if x < PX else x_in[1])

    def powers(head, work, with_dots=False, between=None):
        zero = jnp.zeros((8, LANES), jnp.float32)
        totals = []
        for k in range(1, ITERS + 1):
            h = ITERS - k
            start, count = reach(h)
            prev = head if k == 1 else work[k - 2]
            older = None if k == 1 else head if k == 2 else work[k - 3]
            row = lax.broadcasted_iota(jnp.int32, (count, LANES), 0) + start
            keep = jnp.logical_and(row >= PY, row < PY + rows)
            a, b = zero, zero
            for x in range(PX - h, PX + half + h):
                t, centre = stencil(prev, x, start, count)
                ok = inside(x, start, count)
                for z in range(parts):
                    if k == 1:
                        new = t[z] * (1.0 / HALF)
                    else:
                        new = t[z] * (2.0 / HALF) - older[x, z, pl.ds(start, count), :]
                    if h > 0:
                        new = jnp.where(ok, new, 0.0)
                    work[k - 1][x, z, pl.ds(start, count), :] = new
                    if with_dots and PX <= x < PX + half:
                        square, cross = centre[z] * centre[z], centre[z] * new
                        if h > 0:
                            square, cross = jnp.where(keep, square, 0.0), jnp.where(keep, cross, 0.0)
                        a = a + fold(square)
                        b = b + fold(cross)
            totals += [a, b]
            if between is not None:
                between(k)
        return totals

    def position(axes):
        flat = 0
        for a in axes:
            flat = flat * lax.axis_size(a) + lax.axis_index(a)
        return flat

    def reduce_all(accs, turn, outgoing, meanwhile):
        n = len(accs)
        size = -(-n // 8) * 8
        eye = lax.broadcasted_iota(jnp.int32, (size, LANES), 0) == lax.broadcasted_iota(jnp.int32, (size, LANES), 1)
        tall = jnp.concatenate([jnp.sum(a, axis=0, keepdims=True) for a in accs]
                               + [jnp.zeros((size - n, LANES), jnp.float32)] * (size > n), axis=0)
        col = jnp.sum(tall, axis=1, keepdims=True)
        line = jnp.sum(jnp.where(eye, col, 0.0), axis=0, keepdims=True)
        for s, axes in enumerate(stages):
            count = 1
            for a in axes:
                count *= lax.axis_size(a)
            me = position(axes)
            cell = slots[s].at[turn, pl.ds(me, 1), :]
            cell[...] = line
            copies = []
            for off in range(1, count):
                peer = lax.rem(me + off, count)
                ids = {}
                for a in reversed(axes):
                    ids[a] = lax.rem(peer, lax.axis_size(a))
                    peer = lax.div(peer, lax.axis_size(a))
                copy = pltpu.make_async_remote_copy(
                    src_ref=cell, dst_ref=cell, send_sem=red_send[s].at[turn, off - 1],
                    recv_sem=red_recv[s].at[turn, off - 1], device_id=ids, device_id_type=MESH)
                copy.start()
                copies.append(copy)
            if s == 0:
                for item in outgoing:
                    send_halo(*item)
            if s == len(stages) - 1:
                meanwhile()
            for copy in copies:
                copy.wait_recv()
            line = jnp.sum(slots[s][turn], axis=0, keepdims=True)
            for copy in copies:
                copy.wait_send()
            if s == 0 and turn == 0:
                meet(5)
        col = jnp.sum(jnp.where(eye, line, 0.0), axis=1, keepdims=True)
        wide = jnp.broadcast_to(col, (size, LANES))
        return [jnp.broadcast_to(wide[k:k + 1, :], (8, LANES)) for k in range(n)]

    def place(ref, f, part, z):
        return ref.at[0, pl.ds(part * half, half), :, slice(z * LANES, (z + 1) * LANES)]

    def piece(f, z):
        return pltpu.make_async_copy(result.at[f, :, z], place(out_ref, f, level, z), out_sem.at[z])

    def across(f, z):
        return pltpu.make_async_remote_copy(
            src_ref=result.at[f, :, z], dst_ref=place(out_ref, f, level, z), send_sem=p_send.at[z], recv_sem=p_recv.at[z],
            device_id={"level": f, "gx": gx, "yz": yz}, device_id_type=MESH)

    def deliver(f):
        for z in range(parts):
            pl.when(level != f)(lambda z=z: across(f, z).start())
            pl.when(level == f)(lambda z=z: piece(f, z).start())

    pl.semaphore_wait(barrier, greeted)
    meet(0)
    starts = ((p0, PX, 0), (dmp, PX - 1, 1), (src, PX - 1, 2))
    for item, at in zip(starts, (0, 2, 1)):
        for copy in loads[at * parts:(at + 1) * parts]:
            copy.wait()
        send_halo(*item)
    for item in starts:
        wait_halo(*item)
    meet(1)

    start, count = reach(ITERS)
    for x in range(PX - ITERS, PX + half + ITERS):
        t, centre = stencil(p0, x, start, count)
        ok = inside(x, start, count)
        for z in range(parts):
            r = src[x, z, pl.ds(start, count), :] - (t[z] + (MID - 1.0) * centre[z])
            first[0, x, z, pl.ds(start, count), :] = jnp.where(ok, r, 0.0)
    meet(2)
    accs = powers(first.at[0], (first.at[1], first.at[2], heads_p.at[0]), True,
                  lambda k: meet(k + 2) if k < ITERS else None)

    pending = list(starts)
    slot = len(starts)
    for turn in range(STEPS + 1):
        with_p, with_c = turn < STEPS, turn > 0
        outgoing, jobs = [], []
        if with_p:
            outgoing.append((heads_p.at[turn], ITERS, slot))
            jobs.append((heads_p.at[turn], work_p))
            slot += 1
        if with_p and with_c:
            outgoing.append((heads_c.at[turn - 1], ITERS, slot))
            jobs.append((heads_c.at[turn - 1], work_c))
            slot += 1

        def meanwhile(outgoing=outgoing, jobs=jobs):
            for item, (head, work) in zip(outgoing, jobs):
                wait_halo(*item)
                powers(head, [work.at[k] for k in range(ITERS)])

        pending += outgoing
        dots = reduce_all(accs, turn, outgoing, meanwhile)
        sets = [cg_coefficients(dots[6 * i:6 * i + 6]) for i in range(len(dots) // 6)]
        if with_p:
            rise_p, table_p = sets[0][0], shifted(sets[0][1])
        if with_c:
            rise_c, table_c = sets[-1][0], shifted(sets[-1][1])
        n_acc = 6 * ((turn + 1 < STEPS) + (turn < STEPS))

        def update(i, accs):
            x = i + PX
            accs = list(accs)
            for z in range(parts):
                for y in range(0, rows, 8):
                    near, wide = pl.ds(y, 8), pl.ds(PY + y, 8)
                    if with_p:
                        if turn == 0:
                            v = [first[j, x, z, wide, :] for j in range(ITERS)]
                        else:
                            v = [own_p[j, i, z, near, :] for j in range(ITERS)]
                        v.append(heads_p[turn, x, z, wide, :])
                        v += [work_p[k, x, z, wide, :] for k in range(ITERS)]
                        before = p0[x, z, wide, :] if turn == 0 else sums[0, i, z, near, :]
                        after = before + combine(rise_p, v)
                        if turn + 1 < STEPS:
                            sums[0, i, z, near, :] = after
                        else:
                            result[0, i, z, near, :] = after
                        change = [combine(row, v) for row in table_p]
                    if with_c:
                        u = [own_c[j, i, z, near, :] for j in range(ITERS)]
                        before = p0[x, z, wide, :] if turn == 1 else sums[1, i, z, near, :]
                        after = before + combine(rise_c, u)
                        if turn < STEPS:
                            sums[1, i, z, near, :] = after
                            u.append(heads_c[turn - 1, x, z, wide, :])
                            u += [work_c[k, x, z, wide, :] for k in range(ITERS)]
                        else:
                            result[1, i, z, near, :] = after
                    if turn == STEPS:
                        continue
                    news = []
                    if turn + 1 < STEPS:
                        fresh = [a - b for a, b in zip(v, change)]
                        for j in range(ITERS):
                            own_p[j, i, z, near, :] = fresh[j]
                        heads_p[turn + 1, x, z, wide, :] = fresh[ITERS]
                        news.append(fresh)
                    if turn == 0:
                        ground = v[:ITERS + 1]
                    else:
                        if turn == 1:
                            ground = [first[j, x, z, wide, :] for j in range(ITERS)] + [heads_p[0, x, z, wide, :]]
                        else:
                            ground = [base[j, i, z, near, :] for j in range(ITERS + 1)]
                        ground = [a - combine(row, u) for a, row in zip(ground, table_c)]
                        if turn + 1 < STEPS:
                            for j in range(ITERS + 1):
                                base[j, i, z, near, :] = ground[j]
                    fresh = [a + 0.5 * b for a, b in zip(ground, change)]
                    for j in range(ITERS):
                        own_c[j, i, z, near, :] = fresh[j]
                    heads_c[turn, x, z, wide, :] = fresh[ITERS]
                    news.append(fresh)
                    for f, fresh in enumerate(news):
                        for j in range(ITERS):
                            accs[6 * f + 2 * j] = accs[6 * f + 2 * j] + fresh[j] * fresh[j]
                            accs[6 * f + 2 * j + 1] = accs[6 * f + 2 * j + 1] + fresh[j] * fresh[j + 1]
            return tuple(accs)

        accs = lax.fori_loop(0, half, update, (jnp.zeros((8, LANES), jnp.float32),) * n_acc)
        if turn == STEPS - 1:
            deliver(0)
    deliver(1)
    for item in pending:
        end_halo(*item)
    for f in range(2):
        for z in range(parts):
            pl.when(level != f)(lambda f=f, z=z: across(f, z).wait_send())
            pl.when(level == f)(lambda f=f, z=z: across(f, z).wait_recv())
            pl.when(level == f)(lambda f=f, z=z: piece(f, z).wait())


def solution(mesh):
    levels, nx, ny = mesh.shape["level"], mesh.shape["gx"], mesh.shape["yz"]
    stages = (("level", "gx"), ("yz",))

    def per_device(init_field, source, damping):
        deep, rows, wide = init_field.shape
        half, parts = deep // levels, wide // LANES
        padded = (half + 2 * PX, parts, rows + 2 * PY, LANES)
        plain = (half, parts, rows, LANES)
        counts = []
        for axes in stages:
            n = 1
            for a in axes:
                n *= mesh.shape[a]
            counts.append(n)
        turns = STEPS + 1
        dma = pltpu.SemaphoreType.DMA
        exchanges = 3 + 2 * STEPS - 1
        vmem = lambda n, shape: pltpu.VMEM((n,) + shape, jnp.float32)
        return pl.pallas_call(
            functools.partial(body, (levels, nx, ny), stages),
            out_shape=jax.ShapeDtypeStruct((1, deep, rows, wide), jnp.float32),
            in_specs=[pl.BlockSpec(memory_space=pl.ANY)] * 3,
            out_specs=pl.BlockSpec(memory_space=pl.ANY),
            scratch_shapes=[
                pltpu.VMEM(padded, jnp.float32),
                pltpu.VMEM(padded, jnp.float32),
                pltpu.VMEM(padded, jnp.float32),
                vmem(ITERS, padded),
                vmem(STEPS, padded),
                vmem(STEPS, padded),
                vmem(ITERS, plain),
                vmem(ITERS, plain),
                vmem(ITERS + 1, plain),
                vmem(ITERS, padded),
                vmem(ITERS, padded),
                vmem(2, plain),
                vmem(2, plain),
                [pltpu.VMEM((turns, n, LANES), jnp.float32) for n in counts],
                dma((3, parts)),
                dma((exchanges, 8)),
                dma((exchanges, 8)),
                [dma((turns, n - 1)) for n in counts],
                [dma((turns, n - 1)) for n in counts],
                dma((parts,)),
                dma((parts,)),
                dma((parts,)),
                pltpu.SemaphoreType.REGULAR((ROUNDS[0],)),
                pltpu.SemaphoreType.REGULAR((ROUNDS[1],)),
            ],
            compiler_params=pltpu.CompilerParams(has_side_effects=True, collective_id=0),
        )(init_field, source, damping)

    spec = P("gx", "yz", None)
    return jax.shard_map(
        per_device, mesh=mesh, in_specs=(spec, spec, spec),
        out_specs=P("level", "gx", "yz", None), check_vma=False,
    )
```

time: 88.5 us -> 73 us (0.82)
  Pallas kernels: 86.4 us -> 71 us
    pallas_call x1, Pallas kernels: 86.4 us -> 71 us  [per_device(): pl.pallas_call(functools.partial(body, (levels, nx, ny), stages), out_sha...]
where the time goes in v1:
time: 73 us; the launch traced here: 72.9 us
  Pallas kernels  71 us (97%)
  local copies, waits for them, and re-layouts  1.87 us (3%)
    pallas_call x1, Pallas kernels, per_device(): pl.pallas_call(functools.partial(body, (levels, nx, ny), stages), out_sha...  71 us
    unnamed x1, local copies, waits for them, and re-layouts  1.87 us

profile of v1, /device:TPU:1, one launch (start us, length us, event | category | flops | bytes accessed | tf_op | source)
XLA Modules:
  0.0 72.9 jit_solution(12319179894783911411)
XLA Ops:
  0.0 71.0 %shard_map.37 = f32[1,32,16,256]{3,2,1,0:T(8,128)} custom-call(f32[32,16,256]{2,1,0:T(8,128)} %init_ref.1, f32[32,16,256]{2,1,0:T(8,128)} %source_ref.1, f32[32,16,256]{2,1,0:T(8,128)} %damp_ref.1), custom_call_target="tpu_custom_call" | custom-call | tf_op jit(solution)/shard_map/pallas_call | solution.py:492
  71.0 1.9 %copy.5 = f32[1,32,16,256]{3,2,1,0:T(8,128)} copy(f32[1,32,16,256]{3,2,1,0:T(8,128)} %shard_map.37) | data formatting | bytes 1048576

commit v2 on v1

--- a/solution.py
+++ b/solution.py
@@ -9,7 +9,8 @@
 
 STEPS = 3
 ITERS = 3
-ROUNDS = (3, 5)
+ROUNDS = 5
+INNER = 4
 PX = 4
 PY = 8
 LANES = 128
@@ -101,9 +102,9 @@
     return total
 
 
-def body(sizes, stages, init_ref, source_ref, damp_ref, out_ref, p0, src, dmp, first, heads_p, heads_c, own_p, own_c,
-         base, work_p, work_c, sums, result, slots, in_sem, send_sem, recv_sem, red_send, red_recv, out_sem, p_send, p_recv,
-         meet_x, meet_y):
+def body(sizes, init_ref, source_ref, damp_ref, out_ref, p0, src, dmp, first, heads_p, heads_c, own_p, own_c,
+         base, work_p, work_c, sums, result, slots, in_sem, send_sem, recv_sem, red_send, red_recv, p_send, p_recv,
+         met):
     levels, nx, ny = sizes
     half = own_p.shape[1]
     parts = p0.shape[1]
@@ -148,20 +149,16 @@
 
     def meet(turn):
         if turn > 0:
-            for sem, rounds, axis in ((meet_x, ROUNDS[0], 0), (meet_y, ROUNDS[1], 1)):
-                if turn <= rounds:
-                    far = 2 ** (turn - 1)
-                    count = 0
-                    for d in (-far, far):
-                        count = count + jnp.where(exists(*((d, 0) if axis == 0 else (0, d))), 1, 0)
-                    pl.semaphore_wait(sem.at[turn - 1], count)
-        for sem, rounds, axis in ((meet_x, ROUNDS[0], 0), (meet_y, ROUNDS[1], 1)):
-            if turn < rounds:
-                far = 2 ** turn
-                signal_all(sem.at[turn], [(d, 0) if axis == 0 else (0, d) for d in (-far, far)])
+            far = 2 ** (turn - 1)
+            count = 0
+            for d in (-far, far):
+                count = count + jnp.where(exists(0, d), 1, 0)
+            pl.semaphore_wait(met.at[turn - 1], count)
+        if turn < ROUNDS:
+            signal_all(met.at[turn], [(0, -2 ** turn), (0, 2 ** turn)])
 
     barrier = pltpu.get_barrier_semaphore()
-    greeted = signal_all(barrier, DIRS)
+    greeted = signal_all(barrier, DIRS + tuple((d, 0) for d in range(1 - xcount, xcount) if abs(d) > 1))
 
     zero_x = jnp.zeros((PX,) + tuple(p0.shape[1:]), jnp.float32)
     zero_y = jnp.zeros((p0.shape[0], parts, PY, LANES), jnp.float32)
@@ -248,7 +245,7 @@
             return ok
         return jnp.logical_and(ok, x_in[0] if x < PX else x_in[1])
 
-    def powers(head, work, with_dots=False, between=None):
+    def powers(head, work, with_dots=False):
         zero = jnp.zeros((8, LANES), jnp.float32)
         totals = []
         for k in range(1, ITERS + 1):
@@ -277,15 +274,38 @@
                         a = a + fold(square)
                         b = b + fold(cross)
             totals += [a, b]
-            if between is not None:
-                between(k)
         return totals
 
-    def position(axes):
-        flat = 0
+    inner = INNER if ny % INNER == 0 else 1
+    extent = {"level": levels, "gx": nx, "outer": ny // inner, "inner": inner}
+    here = {"level": level, "gx": gx, "outer": lax.div(yz, inner), "inner": lax.rem(yz, inner)}
+    ring = {a: [here[a]] + [lax.rem(here[a] + off, n) for off in range(1, n)] for a, n in extent.items()}
+    flows = []
+    for axes in (("level",), ("gx", "outer", "inner")):
+        peers, me, n = [{}], 0, 1
         for a in axes:
-            flat = flat * lax.axis_size(a) + lax.axis_index(a)
-        return flat
+            peers = [dict(p, **{a: off}) for p in peers for off in range(extent[a])]
+            me, n = me * extent[a] + here[a], n * extent[a]
+        peers = [p for p in peers if any(p.values())]
+        peers.sort(key=lambda p: -sum(min(off, extent[a] - off) for a, off in p.items()))
+        flows.append((peers, me, n))
+
+    def cast(s, turn):
+        peers, me, n = flows[s]
+        copies = []
+        for p in peers:
+            at = {a: ring[a][p.get(a, 0)] for a in extent}
+            cell = slots[s].at[turn, pl.ds(me, 1), :]
+            copies.append(pltpu.make_async_remote_copy(
+                src_ref=cell, dst_ref=cell, send_sem=red_send[s].at[turn], recv_sem=red_recv[s].at[turn],
+                device_id={"level": at["level"], "gx": at["gx"], "yz": at["outer"] * inner + at["inner"]}, device_id_type=MESH))
+        return copies
+
+    def gathered(s, turn):
+        bulk = slots[s].at[turn, pl.ds(0, flows[s][2] - 1), :]
+        return pltpu.make_async_remote_copy(
+            src_ref=bulk, dst_ref=bulk, send_sem=red_send[s].at[turn], recv_sem=red_recv[s].at[turn],
+            device_id={"level": 1 - level, "gx": gx, "yz": yz}, device_id_type=MESH)
 
     def reduce_all(accs, turn, outgoing, meanwhile):
         n = len(accs)
@@ -295,46 +315,24 @@
                                + [jnp.zeros((size - n, LANES), jnp.float32)] * (size > n), axis=0)
         col = jnp.sum(tall, axis=1, keepdims=True)
         line = jnp.sum(jnp.where(eye, col, 0.0), axis=0, keepdims=True)
-        for s, axes in enumerate(stages):
-            count = 1
-            for a in axes:
-                count *= lax.axis_size(a)
-            me = position(axes)
-            cell = slots[s].at[turn, pl.ds(me, 1), :]
-            cell[...] = line
-            copies = []
-            for off in range(1, count):
-                peer = lax.rem(me + off, count)
-                ids = {}
-                for a in reversed(axes):
-                    ids[a] = lax.rem(peer, lax.axis_size(a))
-                    peer = lax.div(peer, lax.axis_size(a))
-                copy = pltpu.make_async_remote_copy(
-                    src_ref=cell, dst_ref=cell, send_sem=red_send[s].at[turn, off - 1],
-                    recv_sem=red_recv[s].at[turn, off - 1], device_id=ids, device_id_type=MESH)
+        for s in range(len(flows)):
+            slots[s][turn, pl.ds(flows[s][1], 1), :] = line
+            for copy in cast(s, turn):
                 copy.start()
-                copies.append(copy)
-            if s == 0:
+            if s == 0 and turn == 0:
+                meet(ROUNDS)
+            if s == len(flows) - 1:
                 for item in outgoing:
                     send_halo(*item)
-            if s == len(stages) - 1:
                 meanwhile()
-            for copy in copies:
-                copy.wait_recv()
+            gathered(s, turn).wait_recv()
             line = jnp.sum(slots[s][turn], axis=0, keepdims=True)
-            for copy in copies:
-                copy.wait_send()
-            if s == 0 and turn == 0:
-                meet(5)
         col = jnp.sum(jnp.where(eye, line, 0.0), axis=1, keepdims=True)
         wide = jnp.broadcast_to(col, (size, LANES))
         return [jnp.broadcast_to(wide[k:k + 1, :], (8, LANES)) for k in range(n)]
 
     def place(ref, f, part, z):
         return ref.at[0, pl.ds(part * half, half), :, slice(z * LANES, (z + 1) * LANES)]
-
-    def piece(f, z):
-        return pltpu.make_async_copy(result.at[f, :, z], place(out_ref, f, level, z), out_sem.at[z])
 
     def across(f, z):
         return pltpu.make_async_remote_copy(
@@ -342,9 +340,15 @@
             device_id={"level": f, "gx": gx, "yz": yz}, device_id_type=MESH)
 
     def deliver(f):
-        for z in range(parts):
-            pl.when(level != f)(lambda z=z: across(f, z).start())
-            pl.when(level == f)(lambda z=z: piece(f, z).start())
+        @pl.when(level != f)
+        def _():
+            for z in range(parts):
+                across(f, z).start()
+
+        @pl.when(level == f)
+        def _():
+            for z in range(parts):
+                place(out_ref, f, level, z)[...] = result[f, :, z]
 
     pl.semaphore_wait(barrier, greeted)
     meet(0)
@@ -353,9 +357,10 @@
         for copy in loads[at * parts:(at + 1) * parts]:
             copy.wait()
         send_halo(*item)
+    for turn in range(1, ROUNDS):
+        meet(turn)
     for item in starts:
         wait_halo(*item)
-    meet(1)
 
     start, count = reach(ITERS)
     for x in range(PX - ITERS, PX + half + ITERS):
@@ -364,9 +369,7 @@
         for z in range(parts):
             r = src[x, z, pl.ds(start, count), :] - (t[z] + (MID - 1.0) * centre[z])
             first[0, x, z, pl.ds(start, count), :] = jnp.where(ok, r, 0.0)
-    meet(2)
-    accs = powers(first.at[0], (first.at[1], first.at[2], heads_p.at[0]), True,
-                  lambda k: meet(k + 2) if k < ITERS else None)
+    accs = powers(first.at[0], (first.at[1], first.at[2], heads_p.at[0]), True)
 
     pending = list(starts)
     slot = len(starts)
@@ -463,37 +466,33 @@
     deliver(1)
     for item in pending:
         end_halo(*item)
+    for turn in range(STEPS + 1):
+        for s in range(len(flows)):
+            gathered(s, turn).wait_send()
     for f in range(2):
         for z in range(parts):
             pl.when(level != f)(lambda f=f, z=z: across(f, z).wait_send())
             pl.when(level == f)(lambda f=f, z=z: across(f, z).wait_recv())
-            pl.when(level == f)(lambda f=f, z=z: piece(f, z).wait())
 
 
 def solution(mesh):
     levels, nx, ny = mesh.shape["level"], mesh.shape["gx"], mesh.shape["yz"]
-    stages = (("level", "gx"), ("yz",))
 
     def per_device(init_field, source, damping):
         deep, rows, wide = init_field.shape
         half, parts = deep // levels, wide // LANES
         padded = (half + 2 * PX, parts, rows + 2 * PY, LANES)
         plain = (half, parts, rows, LANES)
-        counts = []
-        for axes in stages:
-            n = 1
-            for a in axes:
-                n *= mesh.shape[a]
-            counts.append(n)
+        counts = (levels, nx * ny)
         turns = STEPS + 1
         dma = pltpu.SemaphoreType.DMA
         exchanges = 3 + 2 * STEPS - 1
         vmem = lambda n, shape: pltpu.VMEM((n,) + shape, jnp.float32)
         return pl.pallas_call(
-            functools.partial(body, (levels, nx, ny), stages),
-            out_shape=jax.ShapeDtypeStruct((1, deep, rows, wide), jnp.float32),
-            in_specs=[pl.BlockSpec(memory_space=pl.ANY)] * 3,
-            out_specs=pl.BlockSpec(memory_space=pl.ANY),
+            functools.partial(body, (levels, nx, ny)),
+            out_shape=pltpu.VMEM((1, deep, rows, wide), jnp.float32),
+            in_specs=[pl.BlockSpec(memory_space=pltpu.HBM)] * 3,
+            out_specs=pl.BlockSpec(memory_space=pltpu.VMEM),
             scratch_shapes=[
                 pltpu.VMEM(padded, jnp.float32),
                 pltpu.VMEM(padded, jnp.float32),
@@ -512,13 +511,11 @@
                 dma((3, parts)),
                 dma((exchanges, 8)),
                 dma((exchanges, 8)),
-                [dma((turns, n - 1)) for n in counts],
-                [dma((turns, n - 1)) for n in counts],
+                [dma((turns,)) for n in counts],
+                [dma((turns,)) for n in counts],
                 dma((parts,)),
                 dma((parts,)),
-                dma((parts,)),
-                pltpu.SemaphoreType.REGULAR((ROUNDS[0],)),
-                pltpu.SemaphoreType.REGULAR((ROUNDS[1],)),
+                pltpu.SemaphoreType.REGULAR((ROUNDS,)),
             ],
             compiler_params=pltpu.CompilerParams(has_side_effects=True, collective_id=0),
         )(init_field, source, damping)

time: 73 us -> 61.3 us (0.84)
  Pallas kernels: 71 us -> 60.4 us
  local copies, waits for them, and re-layouts: 1.87 us -> 0.8 us
    pallas_call x1, Pallas kernels: 71 us -> 60.4 us  [per_device(): pl.pallas_call(functools.partial(body, (levels, nx, ny)), out_shape=pltpu...]
    unnamed x1, local copies, waits for them, and re-layouts: 1.87 us -> 0.8 us
where the time goes in v2:
time: 61.3 us; the launch traced here: 61.2 us
  Pallas kernels  60.4 us (99%)
  local copies, waits for them, and re-layouts  0.8 us (1%)
    pallas_call x1, Pallas kernels, per_device(): pl.pallas_call(functools.partial(body, (levels, nx, ny)), out_shape=pltpu...  60.4 us

profile of v2, /device:TPU:1, one launch (start us, length us, event | category | flops | bytes accessed | tf_op | source)
XLA Modules:
  0.0 61.2 jit_solution(4952572689543802518)
XLA Ops:
  0.0 60.4 %shard_map.37 = f32[1,32,16,256]{3,2,1,0:T(8,128)S(1)} custom-call(f32[32,16,256]{2,1,0:T(8,128)} %init_ref.1, f32[32,16,256]{2,1,0:T(8,128)} %source_ref.1, f32[32,16,256]{2,1,0:T(8,128)} %damp_ref.1), custom_call_target="tpu_custom_call" | custom-call | tf_op jit(solution)/shard_map/pallas_call | solution.py:491
  60.4 0.8 %copy.5 = f32[1,32,16,256]{3,2,1,0:T(8,128)} copy(f32[1,32,16,256]{3,2,1,0:T(8,128)S(1)} %shard_map.37) | data formatting | bytes 1048576

commit v3 on v2

--- a/solution.py
+++ b/solution.py
@@ -77,33 +77,27 @@
     return answer, change
 
 
-def shifted(change):
-    table = []
-    for j in range(ITERS + 1):
-        row = [None] * (2 * ITERS + 1)
-        for i, c in enumerate(change):
-            for l in (i + j, abs(i - j)):
-                row[l] = 0.5 * c if row[l] is None else row[l] + 0.5 * c
-        for l in range(1, ITERS + 1):
-            far = row[ITERS + l]
-            if far is not None:
-                near = row[ITERS - l]
-                row[ITERS - l] = -far if near is None else near - far
-                row[ITERS + l] = 2.0 * far
-        table.append(row)
-    return table
+def shifted(c, v):
+    t, w = v[:ITERS + 1], v[ITERS + 1:]
+    one, two = 0.5 * c[1], 0.5 * c[2]
+    even, odd, gap = t[0] + t[2], t[1] + t[3], t[0] - t[2]
+    return [
+        c[0] * t[0] + c[1] * t[1] + (c[2] * t[2] + c[3] * t[3]),
+        c[0] * t[1] + one * even + (two * odd + c[3] * w[0]),
+        c[0] * t[2] + one * odd + (two * gap + c[2] * w[0]) + c[3] * w[1],
+        c[0] * t[3] + c[1] * w[0] + (c[2] * w[1] + c[3] * w[2]),
+    ]
 
 
 def combine(c, v):
     total = None
     for a, b in zip(c, v):
-        if a is not None:
-            total = a * b if total is None else total + a * b
+        total = a * b if total is None else total + a * b
     return total
 
 
 def body(sizes, init_ref, source_ref, damp_ref, out_ref, p0, src, dmp, first, heads_p, heads_c, own_p, own_c,
-         base, work_p, work_c, sums, result, slots, in_sem, send_sem, recv_sem, red_send, red_recv, p_send, p_recv,
+         base, work_p, work_c, sums, result, far_c, slots, in_sem, send_sem, recv_sem, red_send, red_recv, p_send, p_recv, up_send, up_recv,
          met):
     levels, nx, ny = sizes
     half = own_p.shape[1]
@@ -213,7 +207,7 @@
         for k in order:
             pl.when(exists(*DIRS[k]))(lambda k=k: halo_copy(*item, k).wait_send())
 
-    def stencil(v, x, start, count):
+    def around(v, x, start, count):
         lane = lax.broadcasted_iota(jnp.int32, (count, LANES), 1)
         own = pl.ds(start, count)
         centre = [v[x, z, own, :] for z in range(parts)]
@@ -226,8 +220,13 @@
             beside = v[x - 1, z, own, :] + v[x + 1, z, own, :]
             beside = beside + v[x, z, pl.ds(start - 1, count), :] + v[x, z, pl.ds(start + 1, count), :]
             beside = beside + (near + far)
-            out.append((dmp[x, z, own, :] + (7.0 - MID)) * centre[z] - beside)
+            out.append(beside)
         return out, centre
+
+    def stencil(v, x, start, count):
+        out, centre = around(v, x, start, count)
+        own = pl.ds(start, count)
+        return [(dmp[x, z, own, :] + (7.0 - MID)) * centre[z] - out[z] for z in range(parts)], centre
 
     low = jnp.where(y_in[0], 0, PY)
     high = jnp.where(y_in[1], 2 * PY + rows, PY + rows)
@@ -307,7 +306,7 @@
             src_ref=bulk, dst_ref=bulk, send_sem=red_send[s].at[turn], recv_sem=red_recv[s].at[turn],
             device_id={"level": 1 - level, "gx": gx, "yz": yz}, device_id_type=MESH)
 
-    def reduce_all(accs, turn, outgoing, meanwhile):
+    def reduce_all(accs, turn, meanwhile):
         n = len(accs)
         size = -(-n // 8) * 8
         eye = lax.broadcasted_iota(jnp.int32, (size, LANES), 0) == lax.broadcasted_iota(jnp.int32, (size, LANES), 1)
@@ -317,45 +316,63 @@
         line = jnp.sum(jnp.where(eye, col, 0.0), axis=0, keepdims=True)
         for s in range(len(flows)):
             slots[s][turn, pl.ds(flows[s][1], 1), :] = line
-            for copy in cast(s, turn):
-                copy.start()
+
+            def start(s=s):
+                for copy in cast(s, turn):
+                    copy.start()
+
+            def finish(s=s):
+                gathered(s, turn).wait_recv()
+
+            last = s == len(flows) - 1
+            alone = last and turn == STEPS
+            pl.when(level == 1)(start) if alone else start()
             if s == 0 and turn == 0:
                 meet(ROUNDS)
-            if s == len(flows) - 1:
-                for item in outgoing:
-                    send_halo(*item)
+            if last:
                 meanwhile()
-            gathered(s, turn).wait_recv()
+            pl.when(level == 1)(finish) if alone else finish()
             line = jnp.sum(slots[s][turn], axis=0, keepdims=True)
         col = jnp.sum(jnp.where(eye, line, 0.0), axis=1, keepdims=True)
         wide = jnp.broadcast_to(col, (size, LANES))
         return [jnp.broadcast_to(wide[k:k + 1, :], (8, LANES)) for k in range(n)]
 
-    def place(ref, f, part, z):
-        return ref.at[0, pl.ds(part * half, half), :, slice(z * LANES, (z + 1) * LANES)]
-
-    def across(f, z):
+    def place(part, z):
+        return out_ref.at[0, pl.ds(part * half, half), :, slice(z * LANES, (z + 1) * LANES)]
+
+    def across(z):
         return pltpu.make_async_remote_copy(
-            src_ref=result.at[f, :, z], dst_ref=place(out_ref, f, level, z), send_sem=p_send.at[z], recv_sem=p_recv.at[z],
-            device_id={"level": f, "gx": gx, "yz": yz}, device_id_type=MESH)
-
-    def deliver(f):
-        @pl.when(level != f)
+            src_ref=result.at[:, z], dst_ref=place(1, z), send_sem=p_send.at[z], recv_sem=p_recv.at[z],
+            device_id={"level": 0, "gx": gx, "yz": yz}, device_id_type=MESH)
+
+    def upward(k):
+        source, target = ((own_c, far_c.at[0:ITERS]), (sums.at[1], far_c.at[ITERS]))[k]
+        return pltpu.make_async_remote_copy(
+            src_ref=source, dst_ref=target, send_sem=up_send.at[k], recv_sem=up_recv.at[k],
+            device_id={"level": 1, "gx": gx, "yz": yz}, device_id_type=MESH)
+
+    def trade():
+        @pl.when(level == 0)
+        def _():
+            for k in range(2):
+                upward(k).start()
+            for z in range(parts):
+                place(0, z)[...] = result[:, z]
+
+        @pl.when(level == 1)
         def _():
             for z in range(parts):
-                across(f, z).start()
-
-        @pl.when(level == f)
-        def _():
-            for z in range(parts):
-                place(out_ref, f, level, z)[...] = result[f, :, z]
-
+                across(z).start()
+
+    for copy in loads:
+        copy.wait()
+    for x in range(PX, PX + half):
+        for z in range(parts):
+            src[x, z, PY:PY + rows, :] = src[x, z, PY:PY + rows, :] - dmp[x, z, PY:PY + rows, :] * p0[x, z, PY:PY + rows, :]
     pl.semaphore_wait(barrier, greeted)
     meet(0)
-    starts = ((p0, PX, 0), (dmp, PX - 1, 1), (src, PX - 1, 2))
-    for item, at in zip(starts, (0, 2, 1)):
-        for copy in loads[at * parts:(at + 1) * parts]:
-            copy.wait()
+    starts = ((p0, PX, 0), (src, ITERS, 1), (dmp, ITERS - 1, 2))
+    for item in starts:
         send_halo(*item)
     for turn in range(1, ROUNDS):
         meet(turn)
@@ -364,10 +381,10 @@
 
     start, count = reach(ITERS)
     for x in range(PX - ITERS, PX + half + ITERS):
-        t, centre = stencil(p0, x, start, count)
+        t, centre = around(p0, x, start, count)
         ok = inside(x, start, count)
         for z in range(parts):
-            r = src[x, z, pl.ds(start, count), :] - (t[z] + (MID - 1.0) * centre[z])
+            r = src[x, z, pl.ds(start, count), :] - (6.0 * centre[z] - t[z])
             first[0, x, z, pl.ds(start, count), :] = jnp.where(ok, r, 0.0)
     accs = powers(first.at[0], (first.at[1], first.at[2], heads_p.at[0]), True)
 
@@ -375,28 +392,30 @@
     slot = len(starts)
     for turn in range(STEPS + 1):
         with_p, with_c = turn < STEPS, turn > 0
-        outgoing, jobs = [], []
-        if with_p:
-            outgoing.append((heads_p.at[turn], ITERS, slot))
-            jobs.append((heads_p.at[turn], work_p))
-            slot += 1
-        if with_p and with_c:
-            outgoing.append((heads_c.at[turn - 1], ITERS, slot))
-            jobs.append((heads_c.at[turn - 1], work_c))
-            slot += 1
-
-        def meanwhile(outgoing=outgoing, jobs=jobs):
-            for item, (head, work) in zip(outgoing, jobs):
+        jobs = []
+        for on, head, work in ((with_p, heads_p.at[turn], work_p), (with_p and with_c, heads_c.at[turn - 1], work_c)):
+            if on:
+                jobs.append(((head, ITERS, slot), work))
+                slot += 1
+        if jobs:
+            send_halo(*jobs[0][0])
+
+        def meanwhile(turn=turn, jobs=jobs):
+            for item, _ in jobs[1:]:
+                send_halo(*item)
+            if turn == STEPS:
+                trade()
+            for item, work in jobs:
                 wait_halo(*item)
-                powers(head, [work.at[k] for k in range(ITERS)])
-
-        pending += outgoing
-        dots = reduce_all(accs, turn, outgoing, meanwhile)
+                powers(item[0], [work.at[k] for k in range(ITERS)])
+
+        pending += [item for item, _ in jobs]
+        dots = reduce_all(accs, turn, meanwhile)
         sets = [cg_coefficients(dots[6 * i:6 * i + 6]) for i in range(len(dots) // 6)]
         if with_p:
-            rise_p, table_p = sets[0][0], shifted(sets[0][1])
+            rise_p, step_p = sets[0]
         if with_c:
-            rise_c, table_c = sets[-1][0], shifted(sets[-1][1])
+            rise_c, step_c = sets[-1]
         n_acc = 6 * ((turn + 1 < STEPS) + (turn < STEPS))
 
         def update(i, accs):
@@ -417,20 +436,14 @@
                         if turn + 1 < STEPS:
                             sums[0, i, z, near, :] = after
                         else:
-                            result[0, i, z, near, :] = after
-                        change = [combine(row, v) for row in table_p]
+                            result[i, z, near, :] = after
+                        change = shifted(step_p, v)
                     if with_c:
                         u = [own_c[j, i, z, near, :] for j in range(ITERS)]
                         before = p0[x, z, wide, :] if turn == 1 else sums[1, i, z, near, :]
-                        after = before + combine(rise_c, u)
-                        if turn < STEPS:
-                            sums[1, i, z, near, :] = after
-                            u.append(heads_c[turn - 1, x, z, wide, :])
-                            u += [work_c[k, x, z, wide, :] for k in range(ITERS)]
-                        else:
-                            result[1, i, z, near, :] = after
-                    if turn == STEPS:
-                        continue
+                        sums[1, i, z, near, :] = before + combine(rise_c, u)
+                        u.append(heads_c[turn - 1, x, z, wide, :])
+                        u += [work_c[k, x, z, wide, :] for k in range(ITERS)]
                     news = []
                     if turn + 1 < STEPS:
                         fresh = [a - b for a, b in zip(v, change)]
@@ -445,7 +458,7 @@
                             ground = [first[j, x, z, wide, :] for j in range(ITERS)] + [heads_p[0, x, z, wide, :]]
                         else:
                             ground = [base[j, i, z, near, :] for j in range(ITERS + 1)]
-                        ground = [a - combine(row, u) for a, row in zip(ground, table_c)]
+                        ground = [a - b for a, b in zip(ground, shifted(step_c, u))]
                         if turn + 1 < STEPS:
                             for j in range(ITERS + 1):
                                 base[j, i, z, near, :] = ground[j]
@@ -460,19 +473,37 @@
                             accs[6 * f + 2 * j + 1] = accs[6 * f + 2 * j + 1] + fresh[j] * fresh[j + 1]
             return tuple(accs)
 
-        accs = lax.fori_loop(0, half, update, (jnp.zeros((8, LANES), jnp.float32),) * n_acc)
-        if turn == STEPS - 1:
-            deliver(0)
-    deliver(1)
+        def last(i, carry):
+            for z in range(parts):
+                for y in range(0, rows, 8):
+                    near, lanes = pl.ds(y, 8), slice(z * LANES, (z + 1) * LANES)
+                    out_ref[0, half + i, near, lanes] = sums[1, i, z, near, :] + combine(
+                        rise_c, [own_c[j, i, z, near, :] for j in range(ITERS)])
+                    out_ref[0, i, near, lanes] = far_c[ITERS, i, z, near, :] + combine(
+                        rise_c, [far_c[j, i, z, near, :] for j in range(ITERS)])
+            return carry
+
+        if turn < STEPS:
+            accs = lax.fori_loop(0, half, update, (jnp.zeros((8, LANES), jnp.float32),) * n_acc)
+        else:
+            @pl.when(level == 1)
+            def _():
+                for k in range(2):
+                    upward(k).wait_recv()
+                lax.fori_loop(0, half, last, 0)
     for item in pending:
         end_halo(*item)
     for turn in range(STEPS + 1):
-        for s in range(len(flows)):
-            gathered(s, turn).wait_send()
-    for f in range(2):
-        for z in range(parts):
-            pl.when(level != f)(lambda f=f, z=z: across(f, z).wait_send())
-            pl.when(level == f)(lambda f=f, z=z: across(f, z).wait_recv())
+        gathered(0, turn).wait_send()
+        if turn < STEPS:
+            gathered(1, turn).wait_send()
+        else:
+            pl.when(level == 1)(lambda turn=turn: gathered(1, turn).wait_send())
+    for z in range(parts):
+        pl.when(level == 1)(lambda z=z: across(z).wait_send())
+        pl.when(level == 0)(lambda z=z: across(z).wait_recv())
+    for k in range(2):
+        pl.when(level == 0)(lambda k=k: upward(k).wait_send())
 
 
 def solution(mesh):
@@ -506,7 +537,8 @@
                 vmem(ITERS, padded),
                 vmem(ITERS, padded),
                 vmem(2, plain),
-                vmem(2, plain),
+                pltpu.VMEM(plain, jnp.float32),
+                vmem(ITERS + 1, plain),
                 [pltpu.VMEM((turns, n, LANES), jnp.float32) for n in counts],
                 dma((3, parts)),
                 dma((exchanges, 8)),
@@ -515,6 +547,8 @@
                 [dma((turns,)) for n in counts],
                 dma((parts,)),
                 dma((parts,)),
+                dma((2,)),
+                dma((2,)),
                 pltpu.SemaphoreType.REGULAR((ROUNDS,)),
             ],
             compiler_params=pltpu.CompilerParams(has_side_effects=True, collective_id=0),

time: 61.3 us -> 57.4 us (0.936)
  Pallas kernels: 60.4 us -> 56.5 us
    pallas_call x1, Pallas kernels: 60.4 us -> 56.5 us  [per_device(): pl.pallas_call(functools.partial(body, (levels, nx, ny)), out_shape=pltpu...]
where the time goes in v3:
time: 57.4 us; the launch traced here: 57.3 us
  Pallas kernels  56.5 us (98%)
  local copies, waits for them, and re-layouts  0.8 us (1%)
    pallas_call x1, Pallas kernels, per_device(): pl.pallas_call(functools.partial(body, (levels, nx, ny)), out_shape=pltpu...  56.5 us

profile of v3, /device:TPU:1, one launch (start us, length us, event | category | flops | bytes accessed | tf_op | source)
XLA Modules:
  0.0 57.3 jit_solution(9687734326398246930)
XLA Ops:
  0.0 56.5 %shard_map.37 = f32[1,32,16,256]{3,2,1,0:T(8,128)S(1)} custom-call(f32[32,16,256]{2,1,0:T(8,128)} %init_ref.1, f32[32,16,256]{2,1,0:T(8,128)} %source_ref.1, f32[32,16,256]{2,1,0:T(8,128)} %damp_ref.1), custom_call_target="tpu_custom_call" | custom-call | tf_op jit(solution)/shard_map/pallas_call | solution.py:522
  56.5 0.8 %copy.5 = f32[1,32,16,256]{3,2,1,0:T(8,128)} copy(f32[1,32,16,256]{3,2,1,0:T(8,128)S(1)} %shard_map.37) | data formatting | bytes 1048576

commit v4 on v3

--- a/solution.py
+++ b/solution.py
@@ -9,7 +9,7 @@
 
 STEPS = 3
 ITERS = 3
-ROUNDS = 5
+ROUNDS = 3
 INNER = 4
 PX = 4
 PY = 8
@@ -141,18 +141,29 @@
                 pl.semaphore_signal(sem, inc=1, device_id=beside(dx, dy), device_id_type=MESH)
         return count
 
+    inner = INNER if ny % INNER == 0 else 1
+    extent = {"level": levels, "gx": nx, "outer": ny // inner, "inner": inner}
+    here = {"level": level, "gx": gx, "outer": lax.div(yz, inner), "inner": lax.rem(yz, inner)}
+    ring = {a: [here[a]] + [lax.rem(here[a] + off, n) for off in range(1, n)] for a, n in extent.items()}
+    deep = extent["outer"]
+    rounds = ([(0, k) for k in range(1, inner)] + [(1, 0), (deep - 1, 0)],
+              [(1, 0), (2, 0), (deep - 2, 0), (deep - 1, 0)],
+              [(k, 0) for k in range(3, deep - 2)])
+
+    def call(sem, steps):
+        for far, near in steps:
+            pl.semaphore_signal(sem, inc=1, device_id_type=MESH, device_id={
+                "level": level, "gx": gx, "yz": ring["outer"][far] * inner + ring["inner"][near]})
+
     def meet(turn):
         if turn > 0:
-            far = 2 ** (turn - 1)
-            count = 0
-            for d in (-far, far):
-                count = count + jnp.where(exists(0, d), 1, 0)
-            pl.semaphore_wait(met.at[turn - 1], count)
+            pl.semaphore_wait(met.at[turn - 1], len(rounds[turn - 1]))
         if turn < ROUNDS:
-            signal_all(met.at[turn], [(0, -2 ** turn), (0, 2 ** turn)])
+            call(met.at[turn], rounds[turn])
 
     barrier = pltpu.get_barrier_semaphore()
-    greeted = signal_all(barrier, DIRS + tuple((d, 0) for d in range(1 - xcount, xcount) if abs(d) > 1))
+    greeted = signal_all(barrier, DIRS + tuple((d, 0) for d in range(1 - xcount, xcount) if abs(d) > 1)) + len(rounds[0])
+    call(barrier, rounds[0])
 
     zero_x = jnp.zeros((PX,) + tuple(p0.shape[1:]), jnp.float32)
     zero_y = jnp.zeros((p0.shape[0], parts, PY, LANES), jnp.float32)
@@ -275,10 +286,6 @@
             totals += [a, b]
         return totals
 
-    inner = INNER if ny % INNER == 0 else 1
-    extent = {"level": levels, "gx": nx, "outer": ny // inner, "inner": inner}
-    here = {"level": level, "gx": gx, "outer": lax.div(yz, inner), "inner": lax.rem(yz, inner)}
-    ring = {a: [here[a]] + [lax.rem(here[a] + off, n) for off in range(1, n)] for a, n in extent.items()}
     flows = []
     for axes in (("level",), ("gx", "outer", "inner")):
         peers, me, n = [{}], 0, 1
@@ -397,12 +404,10 @@
             if on:
                 jobs.append(((head, ITERS, slot), work))
                 slot += 1
-        if jobs:
-            send_halo(*jobs[0][0])
+        for item, _ in jobs:
+            send_halo(*item)
 
         def meanwhile(turn=turn, jobs=jobs):
-            for item, _ in jobs[1:]:
-                send_halo(*item)
             if turn == STEPS:
                 trade()
             for item, work in jobs:
@@ -484,7 +489,7 @@
             return carry
 
         if turn < STEPS:
-            accs = lax.fori_loop(0, half, update, (jnp.zeros((8, LANES), jnp.float32),) * n_acc)
+            accs = lax.fori_loop(0, half, update, (jnp.zeros((8, LANES), jnp.float32),) * n_acc, unroll=2)
         else:
             @pl.when(level == 1)
             def _():

time: 57.4 us -> 55.3 us (0.963)
  Pallas kernels: 56.5 us -> 54.4 us
    pallas_call x1, Pallas kernels: 56.5 us -> 54.4 us  [per_device(): pl.pallas_call(functools.partial(body, (levels, nx, ny)), out_shape=pltpu...]
where the time goes in v4:
time: 55.3 us; the launch traced here: 55.2 us
  Pallas kernels  54.4 us (98%)
  local copies, waits for them, and re-layouts  0.8 us (1%)
    pallas_call x1, Pallas kernels, per_device(): pl.pallas_call(functools.partial(body, (levels, nx, ny)), out_shape=pltpu...  54.4 us

profile of v4, /device:TPU:1, one launch (start us, length us, event | category | flops | bytes accessed | tf_op | source)
XLA Modules:
  0.0 55.2 jit_solution(4526332171606082652)
XLA Ops:
  0.0 54.4 %shard_map.37 = f32[1,32,16,256]{3,2,1,0:T(8,128)S(1)} custom-call(f32[32,16,256]{2,1,0:T(8,128)} %init_ref.1, f32[32,16,256]{2,1,0:T(8,128)} %source_ref.1, f32[32,16,256]{2,1,0:T(8,128)} %damp_ref.1), custom_call_target="tpu_custom_call" | custom-call | tf_op jit(solution)/shard_map/pallas_call | solution.py:527
  54.4 0.8 %copy.5 = f32[1,32,16,256]{3,2,1,0:T(8,128)} copy(f32[1,32,16,256]{3,2,1,0:T(8,128)S(1)} %shard_map.37) | data formatting | bytes 1048576

commit v5 on v4

--- a/solution.py
+++ b/solution.py
@@ -85,8 +85,11 @@
         c[0] * t[0] + c[1] * t[1] + (c[2] * t[2] + c[3] * t[3]),
         c[0] * t[1] + one * even + (two * odd + c[3] * w[0]),
         c[0] * t[2] + one * odd + (two * gap + c[2] * w[0]) + c[3] * w[1],
-        c[0] * t[3] + c[1] * w[0] + (c[2] * w[1] + c[3] * w[2]),
     ]
+
+
+def lifted(c, t, w):
+    return c[0] * t + c[1] * w[0] + (c[2] * w[1] + c[3] * w[2])
 
 
 def combine(c, v):
@@ -383,7 +386,7 @@
         send_halo(*item)
     for turn in range(1, ROUNDS):
         meet(turn)
-    for item in starts:
+    for item in starts[:2]:
         wait_halo(*item)
 
     start, count = reach(ITERS)
@@ -393,19 +396,24 @@
         for z in range(parts):
             r = src[x, z, pl.ds(start, count), :] - (6.0 * centre[z] - t[z])
             first[0, x, z, pl.ds(start, count), :] = jnp.where(ok, r, 0.0)
+    wait_halo(*starts[2])
     accs = powers(first.at[0], (first.at[1], first.at[2], heads_p.at[0]), True)
 
     pending = list(starts)
     slot = len(starts)
+    plan = []
+    for turn in range(STEPS + 1):
+        jobs = []
+        for on, heads, at, work in ((turn < STEPS, heads_p, turn, work_p), (0 < turn < STEPS, heads_c, turn - 1, work_c)):
+            if on:
+                jobs.append(((heads.at[at], ITERS, slot), work))
+                slot += 1
+        plan.append(jobs)
+    for item, _ in plan[0]:
+        send_halo(*item)
     for turn in range(STEPS + 1):
         with_p, with_c = turn < STEPS, turn > 0
-        jobs = []
-        for on, head, work in ((with_p, heads_p.at[turn], work_p), (with_p and with_c, heads_c.at[turn - 1], work_c)):
-            if on:
-                jobs.append(((head, ITERS, slot), work))
-                slot += 1
-        for item, _ in jobs:
-            send_halo(*item)
+        jobs = plan[turn]
 
         def meanwhile(turn=turn, jobs=jobs):
             if turn == STEPS:
@@ -422,6 +430,30 @@
         if with_c:
             rise_c, step_c = sets[-1]
         n_acc = 6 * ((turn + 1 < STEPS) + (turn < STEPS))
+
+        def top(x, i, z, near, wide):
+            before = heads_p[turn, x, z, wide, :]
+            change = lifted(step_p, before, [work_p[k, x, z, wide, :] for k in range(ITERS)])
+            fresh = []
+            if turn + 1 < STEPS:
+                fresh.append(before - change)
+                heads_p[turn + 1, x, z, wide, :] = fresh[0]
+            ground = before
+            if with_c:
+                ground = heads_p[0, x, z, wide, :] if turn == 1 else base[ITERS, i, z, near, :]
+                ground = ground - lifted(step_c, heads_c[turn - 1, x, z, wide, :],
+                                         [work_c[k, x, z, wide, :] for k in range(ITERS)])
+                if turn + 1 < STEPS:
+                    base[ITERS, i, z, near, :] = ground
+            fresh.append(ground + 0.5 * change)
+            heads_c[turn, x, z, wide, :] = fresh[-1]
+            return fresh
+
+        def lead(i, carry):
+            for z in range(parts):
+                for y in range(0, rows, 8):
+                    top(i + PX, i, z, pl.ds(y, 8), pl.ds(PY + y, 8))
+            return carry
 
         def update(i, accs):
             x = i + PX
@@ -449,29 +481,32 @@
                         sums[1, i, z, near, :] = before + combine(rise_c, u)
                         u.append(heads_c[turn - 1, x, z, wide, :])
                         u += [work_c[k, x, z, wide, :] for k in range(ITERS)]
+                    if turn + 1 < STEPS:
+                        tops = [heads_p[turn + 1, x, z, wide, :], heads_c[turn, x, z, wide, :]]
+                    else:
+                        tops = top(x, i, z, near, wide)
                     news = []
                     if turn + 1 < STEPS:
                         fresh = [a - b for a, b in zip(v, change)]
                         for j in range(ITERS):
                             own_p[j, i, z, near, :] = fresh[j]
-                        heads_p[turn + 1, x, z, wide, :] = fresh[ITERS]
                         news.append(fresh)
                     if turn == 0:
-                        ground = v[:ITERS + 1]
+                        ground = v[:ITERS]
                     else:
                         if turn == 1:
-                            ground = [first[j, x, z, wide, :] for j in range(ITERS)] + [heads_p[0, x, z, wide, :]]
+                            ground = [first[j, x, z, wide, :] for j in range(ITERS)]
                         else:
-                            ground = [base[j, i, z, near, :] for j in range(ITERS + 1)]
+                            ground = [base[j, i, z, near, :] for j in range(ITERS)]
                         ground = [a - b for a, b in zip(ground, shifted(step_c, u))]
                         if turn + 1 < STEPS:
-                            for j in range(ITERS + 1):
+                            for j in range(ITERS):
                                 base[j, i, z, near, :] = ground[j]
                     fresh = [a + 0.5 * b for a, b in zip(ground, change)]
                     for j in range(ITERS):
                         own_c[j, i, z, near, :] = fresh[j]
-                    heads_c[turn, x, z, wide, :] = fresh[ITERS]
                     news.append(fresh)
+                    news = [own + [far] for own, far in zip(news, tops)]
                     for f, fresh in enumerate(news):
                         for j in range(ITERS):
                             accs[6 * f + 2 * j] = accs[6 * f + 2 * j] + fresh[j] * fresh[j]
@@ -488,6 +523,10 @@
                         rise_c, [far_c[j, i, z, near, :] for j in range(ITERS)])
             return carry
 
+        if turn + 1 < STEPS:
+            lax.fori_loop(0, half, lead, 0, unroll=2)
+            for item, _ in plan[turn + 1]:
+                send_halo(*item)
         if turn < STEPS:
             accs = lax.fori_loop(0, half, update, (jnp.zeros((8, LANES), jnp.float32),) * n_acc, unroll=2)
         else:

time: 55.3 us -> 54.3 us (0.982)
  Pallas kernels: 54.4 us -> 53.4 us
    pallas_call x1, Pallas kernels: 54.4 us -> 53.4 us  [per_device(): pl.pallas_call(functools.partial(body, (levels, nx, ny)), out_shape=pltpu...]
where the time goes in v5:
time: 54.3 us; the launch traced here: 54.2 us
  Pallas kernels  53.4 us (98%)
  local copies, waits for them, and re-layouts  0.8 us (1%)
    pallas_call x1, Pallas kernels, per_device(): pl.pallas_call(functools.partial(body, (levels, nx, ny)), out_shape=pltpu...  53.4 us

profile of v5, /device:TPU:1, one launch (start us, length us, event | category | flops | bytes accessed | tf_op | source)
XLA Modules:
  0.0 54.2 jit_solution(11536162164726032032)
XLA Ops:
  0.0 53.4 %shard_map.37 = f32[1,32,16,256]{3,2,1,0:T(8,128)S(1)} custom-call(f32[32,16,256]{2,1,0:T(8,128)} %init_ref.1, f32[32,16,256]{2,1,0:T(8,128)} %source_ref.1, f32[32,16,256]{2,1,0:T(8,128)} %damp_ref.1), custom_call_target="tpu_custom_call" | custom-call | tf_op jit(solution)/shard_map/pallas_call | solution.py:566
  53.4 0.8 %copy.5 = f32[1,32,16,256]{3,2,1,0:T(8,128)} copy(f32[1,32,16,256]{3,2,1,0:T(8,128)S(1)} %shard_map.37) | data formatting | bytes 1048576

commit v6 on v5

--- a/solution.py
+++ b/solution.py
@@ -356,7 +356,7 @@
             device_id={"level": 0, "gx": gx, "yz": yz}, device_id_type=MESH)
 
     def upward(k):
-        source, target = ((own_c, far_c.at[0:ITERS]), (sums.at[1], far_c.at[ITERS]))[k]
+        source, target = ((own_c.at[ITERS * (STEPS % 2):ITERS * (STEPS % 2 + 1)], far_c.at[0:ITERS]), (sums.at[1], far_c.at[ITERS]))[k]
         return pltpu.make_async_remote_copy(
             src_ref=source, dst_ref=target, send_sem=up_send.at[k], recv_sem=up_recv.at[k],
             device_id={"level": 1, "gx": gx, "yz": yz}, device_id_type=MESH)
@@ -401,6 +401,7 @@
 
     pending = list(starts)
     slot = len(starts)
+    settle = None
     plan = []
     for turn in range(STEPS + 1):
         jobs = []
@@ -414,8 +415,11 @@
     for turn in range(STEPS + 1):
         with_p, with_c = turn < STEPS, turn > 0
         jobs = plan[turn]
-
-        def meanwhile(turn=turn, jobs=jobs):
+        now, then = ITERS * (turn % 2), ITERS * ((turn + 1) % 2)
+
+        def meanwhile(turn=turn, jobs=jobs, settle=settle):
+            if settle is not None:
+                lax.fori_loop(0, half, settle, 0, unroll=2)
             if turn == STEPS:
                 trade()
             for item, work in jobs:
@@ -426,7 +430,7 @@
         dots = reduce_all(accs, turn, meanwhile)
         sets = [cg_coefficients(dots[6 * i:6 * i + 6]) for i in range(len(dots) // 6)]
         if with_p:
-            rise_p, step_p = sets[0]
+            step_p = sets[0][1]
         if with_c:
             rise_c, step_c = sets[-1]
         n_acc = 6 * ((turn + 1 < STEPS) + (turn < STEPS))
@@ -465,20 +469,12 @@
                         if turn == 0:
                             v = [first[j, x, z, wide, :] for j in range(ITERS)]
                         else:
-                            v = [own_p[j, i, z, near, :] for j in range(ITERS)]
+                            v = [own_p[now + j, i, z, near, :] for j in range(ITERS)]
                         v.append(heads_p[turn, x, z, wide, :])
                         v += [work_p[k, x, z, wide, :] for k in range(ITERS)]
-                        before = p0[x, z, wide, :] if turn == 0 else sums[0, i, z, near, :]
-                        after = before + combine(rise_p, v)
-                        if turn + 1 < STEPS:
-                            sums[0, i, z, near, :] = after
-                        else:
-                            result[i, z, near, :] = after
                         change = shifted(step_p, v)
                     if with_c:
-                        u = [own_c[j, i, z, near, :] for j in range(ITERS)]
-                        before = p0[x, z, wide, :] if turn == 1 else sums[1, i, z, near, :]
-                        sums[1, i, z, near, :] = before + combine(rise_c, u)
+                        u = [own_c[now + j, i, z, near, :] for j in range(ITERS)]
                         u.append(heads_c[turn - 1, x, z, wide, :])
                         u += [work_c[k, x, z, wide, :] for k in range(ITERS)]
                     if turn + 1 < STEPS:
@@ -489,7 +485,7 @@
                     if turn + 1 < STEPS:
                         fresh = [a - b for a, b in zip(v, change)]
                         for j in range(ITERS):
-                            own_p[j, i, z, near, :] = fresh[j]
+                            own_p[then + j, i, z, near, :] = fresh[j]
                         news.append(fresh)
                     if turn == 0:
                         ground = v[:ITERS]
@@ -504,7 +500,7 @@
                                 base[j, i, z, near, :] = ground[j]
                     fresh = [a + 0.5 * b for a, b in zip(ground, change)]
                     for j in range(ITERS):
-                        own_c[j, i, z, near, :] = fresh[j]
+                        own_c[then + j, i, z, near, :] = fresh[j]
                     news.append(fresh)
                     news = [own + [far] for own, far in zip(news, tops)]
                     for f, fresh in enumerate(news):
@@ -513,12 +509,32 @@
                             accs[6 * f + 2 * j + 1] = accs[6 * f + 2 * j + 1] + fresh[j] * fresh[j + 1]
             return tuple(accs)
 
+        def settle(i, carry, turn=turn, now=now, rise_p=sets[0][0], rise_c=sets[-1][0]):
+            x = i + PX
+            for z in range(parts):
+                for y in range(0, rows, 8):
+                    near, wide = pl.ds(y, 8), pl.ds(PY + y, 8)
+                    if turn == 0:
+                        before, v = p0[x, z, wide, :], [first[j, x, z, wide, :] for j in range(ITERS)]
+                    else:
+                        before, v = sums[0, i, z, near, :], [own_p[now + j, i, z, near, :] for j in range(ITERS)]
+                    after = before + combine(rise_p, v)
+                    if turn + 1 < STEPS:
+                        sums[0, i, z, near, :] = after
+                    else:
+                        result[i, z, near, :] = after
+                    if turn > 0:
+                        before = p0[x, z, wide, :] if turn == 1 else sums[1, i, z, near, :]
+                        sums[1, i, z, near, :] = before + combine(
+                            rise_c, [own_c[now + j, i, z, near, :] for j in range(ITERS)])
+            return carry
+
         def last(i, carry):
             for z in range(parts):
                 for y in range(0, rows, 8):
                     near, lanes = pl.ds(y, 8), slice(z * LANES, (z + 1) * LANES)
                     out_ref[0, half + i, near, lanes] = sums[1, i, z, near, :] + combine(
-                        rise_c, [own_c[j, i, z, near, :] for j in range(ITERS)])
+                        rise_c, [own_c[now + j, i, z, near, :] for j in range(ITERS)])
                     out_ref[0, i, near, lanes] = far_c[ITERS, i, z, near, :] + combine(
                         rise_c, [far_c[j, i, z, near, :] for j in range(ITERS)])
             return carry
@@ -575,8 +591,8 @@
                 vmem(ITERS, padded),
                 vmem(STEPS, padded),
                 vmem(STEPS, padded),
-                vmem(ITERS, plain),
-                vmem(ITERS, plain),
+                vmem(2 * ITERS, plain),
+                vmem(2 * ITERS, plain),
                 vmem(ITERS + 1, plain),
                 vmem(ITERS, padded),
                 vmem(ITERS, padded),

time: 54.3 us -> 54.2 us (level)
  no operation moved by 1% of the time
where the time goes in v6:
time: 54.2 us; the launch traced here: 54.1 us
  Pallas kernels  53.3 us (98%)
  local copies, waits for them, and re-layouts  0.8 us (1%)
    pallas_call x1, Pallas kernels, per_device(): pl.pallas_call(functools.partial(body, (levels, nx, ny)), out_shape=pltpu...  53.3 us

profile of v6, /device:TPU:1, one launch (start us, length us, event | category | flops | bytes accessed | tf_op | source)
XLA Modules:
  0.0 54.1 jit_solution(3654239486884513354)
XLA Ops:
  0.0 53.3 %shard_map.37 = f32[1,32,16,256]{3,2,1,0:T(8,128)S(1)} custom-call(f32[32,16,256]{2,1,0:T(8,128)} %init_ref.1, f32[32,16,256]{2,1,0:T(8,128)} %source_ref.1, f32[32,16,256]{2,1,0:T(8,128)} %damp_ref.1), custom_call_target="tpu_custom_call" | custom-call | tf_op jit(solution)/shard_map/pallas_call | solution.py:582
  53.3 0.8 %copy.5 = f32[1,32,16,256]{3,2,1,0:T(8,128)} copy(f32[1,32,16,256]{3,2,1,0:T(8,128)S(1)} %shard_map.37) | data formatting | bytes 1048576

commit v7 on v6

--- a/solution.py
+++ b/solution.py
@@ -550,7 +550,7 @@
             def _():
                 for k in range(2):
                     upward(k).wait_recv()
-                lax.fori_loop(0, half, last, 0)
+                lax.fori_loop(0, half, last, 0, unroll=4)
     for item in pending:
         end_halo(*item)
     for turn in range(STEPS + 1):

time: 54.2 us -> 54.1 us (level)
  no operation moved by 1% of the time
where the time goes in v7:
time: 54.1 us; the launch traced here: 54 us
  Pallas kernels  53.2 us (98%)
  local copies, waits for them, and re-layouts  0.8 us (1%)
    pallas_call x1, Pallas kernels, per_device(): pl.pallas_call(functools.partial(body, (levels, nx, ny)), out_shape=pltpu...  53.2 us

profile of v7, /device:TPU:1, one launch (start us, length us, event | category | flops | bytes accessed | tf_op | source)
XLA Modules:
  0.0 54.0 jit_solution(8591785247551861679)
XLA Ops:
  0.0 53.2 %shard_map.37 = f32[1,32,16,256]{3,2,1,0:T(8,128)S(1)} custom-call(f32[32,16,256]{2,1,0:T(8,128)} %init_ref.1, f32[32,16,256]{2,1,0:T(8,128)} %source_ref.1, f32[32,16,256]{2,1,0:T(8,128)} %damp_ref.1), custom_call_target="tpu_custom_call" | custom-call | tf_op jit(solution)/shard_map/pallas_call | solution.py:582
  53.2 0.8 %copy.5 = f32[1,32,16,256]{3,2,1,0:T(8,128)} copy(f32[1,32,16,256]{3,2,1,0:T(8,128)S(1)} %shard_map.37) | data formatting | bytes 1048576
